TPU v7x, 256 devices: a whole 4x4x8 slice. The times are simulated.
256 devices in a mesh: tm: 4 (over x), chan: 64 (over z, y, core).
Axes of the slice: x: 4, y: 4, z: 8, core: 2. Of those that a mesh axis runs over, the one named last changes fastest.
Arguments:
- observations: float32 [128, 64, 16384], P('chan', None, 'tm'), may hold values from -6 to 6
- transition: float32 [128, 128, 128], P('chan'), may hold values from -1 to 1, as said below
- obs_map: float32 [128, 64, 128], P('chan'), may hold values from -0.25 to 0.25
- measured_weighting: float32 [128, 64], P('chan'), may hold values from 0.05 to 0.5
- obs_precision: float32 [128, 64], P('chan'), may hold values from 0.3 to 9
- fading: float32 [128, 16384], P('chan', 'tm'), may hold values from 0.5 to 1
Outputs:
- states: float32 [128, 128, 16384], P('chan', None, 'tm')
- batch_nis: float32 [128], P('tm')
Inputs may be any that keep to these rules, and one draw needn't show every extreme that they name: Each channel's transition is symmetric with all eigenvalues of magnitude below one.
All inputs are finite; a program needn't handle non-finite values.
Results may differ from a plain program's by a relative error of at most 0.0003.
Values sent between devices are 32-bit elements; how exact they have to be, the bound alone decides.
No kernel may reach another device: no remote copies, remote signals or barrier semaphores. Data moves between devices by JAX's collectives and lax.ppermute only.
A program may use at most 64 MiB of HBM per device.

v0:
```python
import jax
import jax.numpy as jnp
from jax import lax
from jax.experimental import pallas as pl
from jax.experimental.pallas import tpu as pltpu
from jax.sharding import PartitionSpec as P

LANES = 128
CHUNK = 16
PITCH = 17
BATCH = 128
F32 = jnp.float32
BF16 = jnp.bfloat16
HIGHEST = lax.Precision.HIGHEST


def dot(a, b):
    return jnp.dot(a, b, preferred_element_type=F32)


def exact_dot(a, b):
    return jnp.dot(a, b, preferred_element_type=F32, precision=HIGHEST)


def halves(x):
    high = x.astype(BF16)
    low = (x - high.astype(F32)).astype(BF16)
    return high, low


def packed(m):
    high, low = halves(m)
    return jnp.concatenate([high, low], axis=1)


def side_by_side(x):
    high, low = halves(x)
    return jnp.concatenate([high, low], axis=1)


def thirds(x):
    first = x.astype(BF16)
    rest = x - first.astype(F32)
    second = rest.astype(BF16)
    return first, second, (rest - second.astype(F32)).astype(BF16)


def squared(x):
    a, b, c = thirds(x)
    pair = jnp.concatenate([a, b], axis=1)
    out = dot(pair, jnp.concatenate([pair, pair], axis=0))
    rest = dot(jnp.concatenate([a, c], axis=1), jnp.concatenate([c, a], axis=0))
    return out[:, :LANES] + (out[:, LANES:] + rest)


def times(x, both):
    weights = jnp.concatenate([both, both], axis=0)
    out = dot(side_by_side(x), weights)
    width = out.shape[1] // 2
    return out[:, :width] + out[:, width:]


def before(
    y_hbm, f_hbm, t_hbm, h_hbm, w_hbm,
    ends_ref, sums_ref, phi_ref, pairs_ref, fade_ref, powers_ref, last_ref, closed_ref, double_ref,
    gain_ref, seen_ref,
    yt_ref, inv_ref, tree_ref, treef_ref, y_ref, f_ref, t_ref, h_ref, w_ref, in_sem,
):
    small = [
        pltpu.make_async_copy(source, target, in_sem.at[k])
        for k, (source, target) in enumerate(
            ((f_hbm, f_ref), (t_hbm, t_ref), (h_hbm, h_ref), (w_hbm, w_ref))
        )
    ]
    large = pltpu.make_async_copy(y_hbm, y_ref, in_sem.at[4])
    for copy in small:
        copy.start()
    large.start()
    for copy in small:
        copy.wait()
    frames = y_ref.shape[1]
    blocks = frames // LANES
    chunks = frames // CHUNK
    per_block = LANES // CHUNK
    obs = h_ref.shape[1]
    lane = lax.broadcasted_iota(jnp.int32, (1, LANES), 1)

    for b in range(blocks):
        fade_ref[2 * b : 2 * b + 2, :] = f_ref[:, b * LANES : (b + 1) * LANES]
    run = fade_ref[...]
    shift = 1
    while shift < CHUNK:
        run = jnp.where(lane % CHUNK >= shift, run * pltpu.roll(run, shift, 1), run)
        shift *= 2
    fade_ref[...] = run
    inv_ref[...] = 1.0 / run

    closed, gain = [], []
    for c in range(2):
        t, h = t_ref[c], h_ref[c]
        eye = lax.broadcasted_iota(jnp.int32, (obs, obs), 0) == lax.broadcasted_iota(
            jnp.int32, (obs, obs), 1
        )
        column = jnp.sum(jnp.where(eye, w_ref[c : c + 1, :], 0.0), axis=1, keepdims=True)
        g = column * h
        q = lax.dot_general(
            t, h, (((1,), (1,)), ((), ())), precision=HIGHEST, preferred_element_type=F32
        )
        closed.append(t - exact_dot(q, g))
        gain.append(g)
        closed_ref[c] = closed[c]
        gain_ref[c] = g
        seen_ref[c] = q

    large.wait()
    row = lax.broadcasted_iota(jnp.int32, (per_block, LANES), 0)
    wide = lax.broadcasted_iota(jnp.int32, (per_block, LANES), 1)
    last = wide == row * CHUNK + (CHUNK - 1)
    for b in range(blocks):
        y = y_ref[:, b * LANES : (b + 1) * LANES]
        top = y[:obs] * inv_ref[2 * b : 2 * b + 1, :]
        bottom = y[obs:] * inv_ref[2 * b + 1 : 2 * b + 2, :]
        turned = jnp.concatenate([top, bottom], axis=0).T
        for r in range(per_block):
            at = (b * per_block + r) * PITCH
            yt_ref[at : at + CHUNK, :] = turned[r * CHUNK : (r + 1) * CHUNK]
        for c in range(2):
            value = jnp.where(last, fade_ref[2 * b + c : 2 * b + c + 1, :], 0.0)
            total = jnp.sum(value, axis=1, keepdims=True)
            phi_ref[c, b * per_block : (b + 1) * per_block, :] = jnp.broadcast_to(
                total, (per_block, LANES)
            )

    low_half = lane < obs
    for p in range(CHUNK // 2):
        even = yt_ref[pl.ds(2 * p, chunks, stride=PITCH), :]
        odd = pltpu.roll(yt_ref[pl.ds(2 * p + 1, chunks, stride=PITCH), :], obs, 1)
        pairs_ref[0, p] = side_by_side(jnp.where(low_half, even, odd))
        pairs_ref[1, p] = side_by_side(jnp.where(low_half, odd, even))

    powers = []
    for c in range(2):
        b1, g = closed[c], gain[c]
        power = squared(b1)
        double_ref[c] = power
        gb = times(g, packed(b1))
        stack = jnp.concatenate([gb, g] if c == 0 else [g, gb], axis=0)
        reach = 2
        while reach < CHUNK:
            stack = jnp.concatenate([times(stack, packed(power)), stack], axis=0)
            power = squared(power)
            reach *= 2
        total = jnp.zeros((chunks, 2 * LANES), F32)
        for p in range(CHUNK // 2):
            both = packed(stack[p * LANES : (p + 1) * LANES])
            total = total + dot(pairs_ref[c, p], jnp.concatenate([both, both], axis=0))
        powers.append(power)
        sums_ref[c] = phi_ref[c] * (total[:, :LANES] + total[:, LANES:])

    levels = chunks.bit_length() - 1
    for level in range(levels):
        half = chunks >> (level + 1)
        for c in range(2):
            both = packed(powers[c])
            powers_ref[c, level] = both
            source, factors = (sums_ref, phi_ref) if level == 0 else (tree_ref, treef_ref)
            base = 0 if level == 0 else chunks - 4 * half
            first = source[c, pl.ds(base, half, stride=2), :]
            second = source[c, pl.ds(base + 1, half, stride=2), :]
            f0 = factors[c, pl.ds(base, half, stride=2), :]
            f1 = factors[c, pl.ds(base + 1, half, stride=2), :]
            state = second + f1 * times(first, both)
            at = chunks - 2 * half
            tree_ref[c, at : at + half, :] = state
            treef_ref[c, at : at + half, :] = f0 * f1
            if level == levels - 1:
                last_ref[c] = powers[c]
                ends_ref[c : c + 1, :] = state
                ends_ref[2 + c : 3 + c, :] = f0 * f1
            else:
                powers[c] = squared(powers[c])


def between(
    sums_ref, phi_ref, pairs_ref, fade_ref, powers_ref, last_ref, closed_ref, double_ref, gain_ref,
    seen_ref,
    scan_ref, cum_ref, square_ref, section_ref, stepx_ref, stepe_ref, partx_ref, parte_ref,
    pad_ref, padf_ref, tmp_ref,
):
    chunks = sums_ref.shape[1]
    blocks = chunks * CHUNK // LANES
    per_block = LANES // CHUNK
    obs = gain_ref.shape[1]

    run = fade_ref[...]
    for r in range(per_block):
        moved = pltpu.roll(run, (LANES - r * CHUNK) % LANES, 1) if r else run
        tmp_ref[...] = moved * moved
        for c in range(2):
            square_ref[c, pl.ds(r, blocks, stride=per_block), :] = tmp_ref[
                pl.ds(c, blocks, stride=2), :
            ]

    weights = []
    for c in range(2):
        section_ref[c] = packed(squared(last_ref[c]))
        b1, b2, g, q = closed_ref[c], double_ref[c], gain_ref[c], seen_ref[c]
        gb, bq, gq = exact_dot(g, b1), exact_dot(b1, q), exact_dot(g, q)
        high, low = halves(jnp.concatenate([b1, b2], axis=1))
        stepx_ref[c] = jnp.concatenate([high, high, low], axis=0)
        both = packed(jnp.concatenate([q, bq], axis=1))
        stepe_ref[c] = jnp.concatenate([both, both], axis=0)
        none = jnp.zeros((obs, obs), F32)
        top = jnp.concatenate([g, gb, none, gq], axis=1)
        bottom = jnp.concatenate([jnp.zeros_like(g), g, none, none], axis=1)
        high, low = halves(jnp.concatenate([top, bottom] if c == 0 else [bottom, top], axis=0))
        weights.append(jnp.concatenate([high, high, low], axis=0))
        pad_ref[c, :LANES, :] = jnp.zeros((LANES, LANES), F32)
        padf_ref[c, :LANES, :] = jnp.ones((LANES, LANES), F32)

    levels = powers_ref.shape[1]
    state = [sums_ref[c] for c in range(2)]
    factor = [phi_ref[c] for c in range(2)]
    for p in range(max(levels, CHUNK // 2)):
        for c in range(2):
            if p < levels:
                reach = 1 << p
                pad_ref[c, LANES:, :] = state[c]
                padf_ref[c, LANES:, :] = factor[c]
                moved = pad_ref[c, pl.ds(LANES - reach, chunks), :]
                state[c] = state[c] + factor[c] * times(moved, powers_ref[c, p])
                factor[c] = factor[c] * padf_ref[c, pl.ds(LANES - reach, chunks), :]
            if p < CHUNK // 2:
                y = pairs_ref[c, p]
                out = dot(jnp.concatenate([y, y[:, :LANES]], axis=1), weights[c])
                observed = y[:, :LANES].astype(F32) + y[:, LANES:].astype(F32)
                if c == 1:
                    observed = pltpu.roll(observed, obs, 1)
                partx_ref[c, p] = out[:, : 2 * LANES]
                parte_ref[c, p] = observed - out[:, 2 * LANES :]
    for c in range(2):
        scan_ref[c] = state[c]
        cum_ref[c] = factor[c]


def after(
    one_ref, two_ref, three_ref, scan_ref, cum_ref, square_ref, section_ref, stepx_ref, stepe_ref,
    partx_ref, parte_ref, powers_ref, weight_ref,
    rows_ref, nis_ref,
    carry_ref, pad_ref, xt_ref, sem,
):
    chunks = scan_ref.shape[1]
    blocks = chunks * CHUNK // LANES
    per_block = LANES // CHUNK
    obs = weight_ref.shape[1]
    levels = powers_ref.shape[1]
    position = lax.axis_index("tm")
    some = [(position >= k).astype(F32) for k in (1, 2, 3)]

    x = []
    for c in range(2):
        section = section_ref[c]
        s = [r[c : c + 1, :] * m for r, m in zip((one_ref, two_ref, three_ref), some)]
        f = [r[2 + c : 3 + c, :] * m for r, m in zip((one_ref, two_ref, three_ref), some)]
        wide = lambda v: jnp.broadcast_to(v, (8, LANES))
        inner = wide(s[1]) + wide(f[1]) * times(wide(s[2]), section)
        entering = wide(s[0]) + wide(f[0]) * times(inner, section)
        carry_ref[c, :8, :] = entering
        for level in range(levels):
            reach = 1 << level
            rows = max(reach, 8)
            moved = times(carry_ref[c, :rows, :], powers_ref[c, level])
            carry_ref[c, pl.ds(reach, rows), :] = moved
        pad_ref[0, :8, :] = jnp.zeros((8, LANES), F32)
        pad_ref[1, :8, :] = jnp.ones((8, LANES), F32)
        pad_ref[0, 8:, :] = scan_ref[c]
        pad_ref[1, 8:, :] = cum_ref[c]
        x.append(
            pad_ref[0, pl.ds(7, chunks), :]
            + pad_ref[1, pl.ds(7, chunks), :] * carry_ref[c, :chunks, :]
        )

    row = lax.broadcasted_iota(jnp.int32, (LANES, LANES), 0)
    col = lax.broadcasted_iota(jnp.int32, (LANES, LANES), 1)
    score = [jnp.zeros((chunks, LANES), F32) for _ in range(2)]
    copies = []
    for p in range(CHUNK // 2):
        for c in range(2):
            both = side_by_side(x[c])
            out = partx_ref[c, p] + dot(
                jnp.concatenate([both, both[:, :LANES]], axis=1), stepx_ref[c]
            )
            seen = dot(both, stepe_ref[c])
            x[c] = out[:, LANES:]
            xt_ref[c, 2 * p] = out[:, :LANES]
            xt_ref[c, 2 * p + 1] = x[c]
            pair = pl.ds(2 * p, 2)
            copy = pltpu.make_async_copy(
                xt_ref.at[c, pair], rows_ref.at[c, pair], sem.at[c, p]
            )
            copy.start()
            copies.append(copy)
            innovation = parte_ref[c, p] - (seen[:, :LANES] + seen[:, LANES:])
            w = weight_ref[c : c + 1, :]
            term = innovation * innovation * jnp.concatenate([w, w], axis=1)
            pick = jnp.where(col == 2 * p + row // obs, 1.0, 0.0).astype(BF16)
            score[c] = score[c] + dot(side_by_side(term), jnp.concatenate([pick, pick], axis=0))

    total = score[0] * square_ref[0] + score[1] * square_ref[1]
    lanes = lax.broadcasted_iota(jnp.int32, (1, LANES), 1)
    total = jnp.where(lanes < CHUNK, total, 0.0)
    per_batch = jnp.sum(total.reshape(blocks, per_block, LANES), axis=1)
    local = lax.dot_general(
        jnp.ones((8, LANES), F32), per_batch, (((1,), (1,)), ((), ())),
        precision=HIGHEST, preferred_element_type=F32,
    )
    nis_ref[...] = jnp.broadcast_to(local[:1][None], nis_ref.shape)
    for copy in copies:
        copy.wait()


def write(rows_ref, fade_ref, out_ref, xt_ref, stage_ref, in_sem, out_sem):
    channels, steps, chunks, _ = rows_ref.shape
    per_block = LANES // CHUNK
    group = 64
    arriving = {}
    for k in range(chunks // group):
        for c in range(channels):
            part = pl.ds(k * group, group)
            arriving[k, c] = pltpu.make_async_copy(
                rows_ref.at[c, :, part], xt_ref.at[c, k], in_sem.at[c, k]
            )
            arriving[k, c].start()
    leaving = []
    for k in range(chunks // group):
        for c in range(channels):
            arriving[k, c].wait()
            flat = xt_ref.at[c, k]
            for b in range(group // per_block):
                tall = jnp.concatenate(
                    [flat[:, b * per_block + i, :] for i in range(per_block)], axis=0
                )
                block = k * (group // per_block) + b
                row = fade_ref[2 * block + c : 2 * block + c + 1, :]
                stage_ref[c, :, block * LANES : (block + 1) * LANES] = tall.T * row
            columns = pl.ds(k * group * CHUNK, group * CHUNK)
            copy = pltpu.make_async_copy(
                stage_ref.at[c, :, columns], out_ref.at[c, :, columns], out_sem.at[c, k]
            )
            copy.start()
            leaving.append(copy)
    for copy in leaving:
        copy.wait()


def per_device(observations, transition, obs_map, measured_weighting, obs_precision, fading):
    channels, obs, frames = observations.shape
    width = transition.shape[1]
    chunks = frames // CHUNK
    levels = chunks.bit_length() - 1
    blocks = frames // LANES
    vmem = pl.BlockSpec(memory_space=pltpu.VMEM)
    spec = jax.ShapeDtypeStruct
    first = [
        spec((2 * channels, width), F32),
        spec((channels, chunks, width), F32),
        spec((channels, chunks, width), F32),
        spec((channels, CHUNK // 2, chunks, 2 * LANES), BF16),
        spec((2 * blocks, LANES), F32),
        spec((channels, levels, width, 2 * width), BF16),
        spec((channels, width, width), F32),
        spec((channels, width, width), F32),
        spec((channels, width, width), F32),
        spec((channels, obs, width), F32),
        spec((channels, width, obs), F32),
    ]
    ends, *kept = pl.pallas_call(
        before,
        out_shape=first,
        in_specs=[pl.BlockSpec(memory_space=pltpu.HBM)] * 5,
        out_specs=[vmem] * len(first),
        scratch_shapes=[
            pltpu.VMEM((chunks * PITCH, LANES), F32),
            pltpu.VMEM((2 * blocks, LANES), F32),
            pltpu.VMEM((channels, chunks, width), F32),
            pltpu.VMEM((channels, chunks, width), F32),
            pltpu.VMEM((channels * obs, frames), F32),
            pltpu.VMEM(fading.shape, F32),
            pltpu.VMEM(transition.shape, F32),
            pltpu.VMEM(obs_map.shape, F32),
            pltpu.VMEM(measured_weighting.shape, F32),
            pltpu.SemaphoreType.DMA((5,)),
        ],
        compiler_params=pltpu.CompilerParams(vmem_limit_bytes=24 << 20),
        name="before",
    )(
        *(
            pltpu.with_memory_space_constraint(a, pltpu.HBM)
            for a in (
                observations.reshape(channels * obs, frames), fading, transition, obs_map,
                measured_weighting,
            )
        )
    )
    fade, powers = kept[3], kept[4]
    second = [
        spec((channels, chunks, width), F32),
        spec((channels, chunks, width), F32),
        spec((channels, chunks, LANES), F32),
        spec((channels, width, 2 * width), BF16),
        spec((channels, 3 * width, 2 * width), BF16),
        spec((channels, 2 * width, 4 * obs), BF16),
        spec((channels, CHUNK // 2, chunks, 2 * width), F32),
        spec((channels, CHUNK // 2, chunks, 2 * obs), F32),
    ]
    made = pl.pallas_call(
        between,
        out_shape=second,
        in_specs=[vmem] * len(kept),
        out_specs=[vmem] * len(second),
        scratch_shapes=[
            pltpu.VMEM((channels, LANES + chunks, width), F32),
            pltpu.VMEM((channels, LANES + chunks, width), F32),
            pltpu.VMEM((2 * blocks, LANES), F32),
        ],
        compiler_params=pltpu.CompilerParams(vmem_limit_bytes=24 << 20),
        cost_estimate=pl.CostEstimate(
            flops=4_000_000_000, bytes_accessed=8_000_000, transcendentals=0
        ),
        name="between",
    )(*kept)
    sections = lax.axis_size("tm")
    arrived = [
        lax.ppermute(ends, "tm", [(i, (i + s) % sections) for i in range(sections)])
        for s in (1, 2, 3)
    ]
    group = lax.axis_size("chan")
    rows, nis = pl.pallas_call(
        after,
        out_shape=[
            pltpu.HBM((channels, CHUNK, chunks, width), F32),
            spec((group, 1, blocks), F32),
        ],
        in_specs=[vmem] * (5 + len(second)),
        out_specs=[pl.BlockSpec(memory_space=pltpu.HBM), vmem],
        scratch_shapes=[
            pltpu.VMEM((channels, chunks + 8, width), F32),
            pltpu.VMEM((2, chunks + 8, width), F32),
            pltpu.VMEM((channels, CHUNK, chunks, width), F32),
            pltpu.SemaphoreType.DMA((channels, CHUNK // 2)),
        ],
        compiler_params=pltpu.CompilerParams(vmem_limit_bytes=24 << 20),
        cost_estimate=pl.CostEstimate(
            flops=4_000_000_000, bytes_accessed=8_000_000, transcendentals=0
        ),
        name="after",
    )(*arrived, *made, powers, obs_precision)
    everything = lax.all_to_all(nis, "chan", split_axis=0, concat_axis=0, tiled=True)
    states = pl.pallas_call(
        write,
        out_shape=jax.ShapeDtypeStruct((channels, width, frames), F32),
        in_specs=[pl.BlockSpec(memory_space=pltpu.HBM), vmem],
        out_specs=pl.BlockSpec(memory_space=pltpu.HBM),
        scratch_shapes=[
            pltpu.VMEM((channels, chunks // 64, CHUNK, 64, width), F32),
            pltpu.VMEM((channels, width, frames), F32),
            pltpu.SemaphoreType.DMA((channels, chunks // 64)),
            pltpu.SemaphoreType.DMA((channels, chunks // 64)),
        ],
        compiler_params=pltpu.CompilerParams(vmem_limit_bytes=16 << 20),
        cost_estimate=pl.CostEstimate(
            flops=4_000_000_000, bytes_accessed=8 * channels * width * frames, transcendentals=0
        ),
        name="write",
    )(pltpu.with_memory_space_constraint(rows, pltpu.HBM), fade)
    divisor = channels * lax.axis_size("chan") * BATCH * obs
    return states, jnp.sum(everything, axis=(0, 1)) / divisor


def solution(mesh):
    in_specs = (
        P("chan", None, "tm"),
        P("chan", None, None),
        P("chan", None, None),
        P("chan", None),
        P("chan", None),
        P("chan", "tm"),
    )
    out_specs = (P("chan", None, "tm"), P("tm"))
    return jax.shard_map(
        per_device, mesh=mesh, in_specs=in_specs, out_specs=out_specs, check_vma=False
    )
```

profile of v0, /device:TPU:1, one launch (start us, length us, event | category | flops | bytes accessed | tf_op | source)
XLA Modules:
  0.0 44.5 jit_solution(15924896090041908410)
XLA Ops:
  0.6 6.0 %before.1 = (f32[4,128]{1,0:T(4,128)S(1)}, f32[2,256,128]{2,1,0:T(8,128)S(1)}, f32[2,256,128]{2,1,0:T(8,128)S(1)}, bf16[2,8,256,256]{3,2,1,0:T(8,128)(2,1)S(1)},...) custom-call(f32[128,4096]{1,0:T(8,128)} %bitcast.1, ...), custom_call_target="tpu_custom_call" | custom-call | tf_op jit(solution)/shard_map/before/pallas_call | solution.py:377
  6.7 3.4 %collective-permute-start.2 = (f32[4,128]{1,0:T(4,128)S(1)}, f32[4,128]{1,0:T(4,128)S(1)}, u32[]{:S(2)}, u32[]{:S(2)}) collective-permute-start(f32[4,128]{1,0:T(4,128)S(1)} %get-tuple-element.23), channel_id=1, source_target_pairs={{0,192},{64,0},{128,64},{192,128},{1,193},{65,1},{129,65},{193,129... | collective-permute-start | bytes 6152 | tf_op jit(solution)/shard_map/ppermute | solution.py:434
  10.1 0.5 %collective-permute-start.1 = (f32[4,128]{1,0:T(4,128)S(1)}, f32[4,128]{1,0:T(4,128)S(1)}, u32[]{:S(2)}, u32[]{:S(2)}) collective-permute-start(f32[4,128]{1,0:T(4,128)S(1)} %get-tuple-element.23), channel_id=1, source_target_pairs={{0,128},{64,192},{128,0},{192,64},{1,129},{65,193},{129,1},{193,65... | collective-permute-start | bytes 6152 | tf_op jit(solution)/shard_map/ppermute | solution.py:434
  10.6 0.6 %collective-permute-start = (f32[4,128]{1,0:T(4,128)S(1)}, f32[4,128]{1,0:T(4,128)S(1)}, u32[]{:S(2)}, u32[]{:S(2)}) collective-permute-start(f32[4,128]{1,0:T(4,128)S(1)} %get-tuple-element.23), channel_id=1, source_target_pairs={{0,64},{64,128},{128,192},{192,0},{1,65},{65,129},{129,193},{193,1... | collective-permute-start | bytes 6152 | tf_op jit(solution)/shard_map/ppermute | solution.py:434
  11.2 0.0 copy-start
  11.2 3.1 %between.1 = (f32[2,256,128]{2,1,0:T(8,128)S(1)}, f32[2,256,128]{2,1,0:T(8,128)S(1)}, f32[2,256,128]{2,1,0:T(8,128)S(1)}, bf16[2,128,256]{2,1,0:T(8,128)(2,1)S(1...) custom-call(f32[2,256,128]{2,1,0:T(8,128)S(1)} %get-tuple-element.24, ...), custom_call_target="tpu_custom_call" | custom-call | flops 4000000000 | bytes 8000000 | tf_op jit(solution)/shard_map/between/pallas_call | solution.py:416
  14.3 0.0 collective-permute-done.2.three_ref
  14.3 0.0 collective-permute-done.1.two_ref
  14.3 0.0 collective-permute-done.one_ref
  14.3 0.0 copy-done
  14.3 6.2 %after.1 = (f32[2,16,256,128]{3,2,1,0:T(8,128)}, f32[64,1,32]{2,1,0:T(1,128)}) custom-call(f32[4,128]{1,0:T(4,128)S(1)} %collective-permute-done.one_ref, f32[4,128]{1,0:T(4,128)S(1)} %collective-permute-done.1.two_ref, f32[4,128]{1,0:T(4,128)S(1)} %collective-permute-done.2.three_ref, f32[2,256,128]{2,1,0:T(8,128)S(1)} %get-tuple-element.34.scan_ref, ...), custom_call_target="tpu_custom_call" | custom-call | flops 4000000000 | bytes 8000000 | tf_op jit(solution)/shard_map/after/pallas_call | solution.py:438
  20.6 13.9 %all-to-all-start = ((f32[64,1,32]{2,1,0:T(1,128)}), f32[64,1,32]{2,1,0:T(1,128)S(1)}, u32[]{:S(2)}, u32[]{:S(2)}) async-start(f32[64,1,32]{2,1,0:T(1,128)} %get-tuple-element.43), calls=%async_computation | async-start | bytes 65536 | tf_op jit(solution)/shard_map/all_to_all | solution.py:458
  34.5 4.8 %write.1 = f32[2,128,4096]{2,1,0:T(8,128)} custom-call(f32[2,16,256,128]{3,2,1,0:T(8,128)} %get-tuple-element.42.rows_ref, f32[64,128]{1,0:T(8,128)S(1)} %get-tuple-element.27.fade_ref), custom_call_target="tpu_custom_call" | custom-call | flops 4000000000 | bytes 8388608 | tf_op jit(solution)/shard_map/write/pallas_call | solution.py:459
  39.3 4.6 %all-to-all-done = f32[64,1,32]{2,1,0:T(1,128)S(1)} async-done(((f32[64,1,32]{2,1,0:T(1,128)}), f32[64,1,32]{2,1,0:T(1,128)S(1)}, u32[]{:S(2)}, u32[]{:S(2)}) %all-to-all-start) | async-done | bytes 8224 | tf_op jit(solution)/shard_map/all_to_all | solution.py:458
  43.9 0.1 reduce_sum.9
  44.0 0.5 %broadcast_multiply_fusion = f32[32]{0:T(128)} fusion(f32[32]{0:T(128)S(1)} %reduce_sum.9), kind=kLoop, calls=%fused_computation | loop fusion | flops 32 | bytes 256 | tf_op jit(solution)/shard_map/div | solution.py:477
Async XLA Ops:
  6.7 7.6 %collective-permute-start.2 = (f32[4,128]{1,0:T(4,128)S(1)}, f32[4,128]{1,0:T(4,128)S(1)}, u32[]{:S(2)}, u32[]{:S(2)}) collective-permute-start(f32[4,128]{1,0:T(4,128)S(1)} %get-tuple-element.23), channel_id=1, source_target_pairs={{0,192},{64,0},{128,64},{192,128},{1,193},{65,1},{129,65},{193,129... | collective-permute-start | bytes 6152 | tf_op jit(solution)/shard_map/ppermute | solution.py:434
  10.1 4.2 %collective-permute-start.1 = (f32[4,128]{1,0:T(4,128)S(1)}, f32[4,128]{1,0:T(4,128)S(1)}, u32[]{:S(2)}, u32[]{:S(2)}) collective-permute-start(f32[4,128]{1,0:T(4,128)S(1)} %get-tuple-element.23), channel_id=1, source_target_pairs={{0,128},{64,192},{128,0},{192,64},{1,129},{65,193},{129,1},{193,65... | collective-permute-start | bytes 6152 | tf_op jit(solution)/shard_map/ppermute | solution.py:434
  10.6 3.7 %collective-permute-start = (f32[4,128]{1,0:T(4,128)S(1)}, f32[4,128]{1,0:T(4,128)S(1)}, u32[]{:S(2)}, u32[]{:S(2)}) collective-permute-start(f32[4,128]{1,0:T(4,128)S(1)} %get-tuple-element.23), channel_id=1, source_target_pairs={{0,64},{64,128},{128,192},{192,0},{1,65},{65,129},{129,193},{193,1... | collective-permute-start | bytes 6152 | tf_op jit(solution)/shard_map/ppermute | solution.py:434
  11.2 3.1 %copy-start = (f32[2,64]{1,0:T(2,128)S(1)}, f32[2,64]{1,0:T(2,128)}, u32[]{:S(2)}) copy-start(f32[2,64]{1,0:T(2,128)} %weight_ref.1) | copy-start | bytes 1540
  20.6 23.3 %all-to-all-start = ((f32[64,1,32]{2,1,0:T(1,128)}), f32[64,1,32]{2,1,0:T(1,128)S(1)}, u32[]{:S(2)}, u32[]{:S(2)}) async-start(f32[64,1,32]{2,1,0:T(1,128)} %get-tuple-element.43), calls=%async_computation | async-start | bytes 65536 | tf_op jit(solution)/shard_map/all_to_all | solution.py:458
where the time goes:
time: 44.7 us; the launch traced here: 44.5 us
  Pallas kernels  20.1 us (45%)
  starting transfers between devices  18.4 us (41%)
  waiting for transfers between devices  4.65 us (10%)
  between operations  0.7 us (2%)
  other arithmetic  0.6 us (1%)
    all_to_all x1, starting transfers between devices, per_device(): lax.all_to_all(nis, 'chan', split_axis=0, concat_axis=0, tiled=True)  13.9 us
    pallas_call x1, Pallas kernels, per_device(): pl.pallas_call(after, out_shape=[pltpu.HBM((channels, CHUNK, chunks, widt...  6.23 us
    pallas_call x1, Pallas kernels, per_device(): pl.pallas_call(before, out_shape=first, in_specs=[pl.BlockSpec(memory_spa...  6.04 us
    pallas_call x1, Pallas kernels, per_device(): pl.pallas_call(write, out_shape=jax.ShapeDtypeStruct((channels, width, fr...  4.76 us
    all_to_all x1, waiting for transfers between devices, per_device(): lax.all_to_all(nis, 'chan', split_axis=0, concat_axis=0, tiled=True)  4.64 us
    ppermute x3, starting transfers between devices, per_device(): lax.ppermute(ends, 'tm', [(i, (i + s) % sections) for i in range(sections)])  4.5 us
    pallas_call x1, Pallas kernels, per_device(): pl.pallas_call(between, out_shape=second, in_specs=[vmem] * len(kept), ou...  3.1 us
  transfers between devices with their start and end apart: 4, of which 1 were waited for; matrix products, arithmetic and copies ran while one was open for 0% of the time, Pallas kernels for 18%

commit v1 on v0

--- a/solution.py
+++ b/solution.py
@@ -58,6 +58,14 @@
     out = dot(side_by_side(x), weights)
     width = out.shape[1] // 2
     return out[:, :width] + out[:, width:]
+
+
+def times_rows(x, both):
+    rows = x.shape[0]
+    high = x.astype(BF16).astype(F32)
+    out = dot(jnp.concatenate([high, x - high], axis=0).astype(BF16), both)
+    out = out[:rows] + out[rows:]
+    return out[:, :LANES] + out[:, LANES:]
 
 
 def before(
@@ -112,6 +120,31 @@
         gain_ref[c] = g
         seen_ref[c] = q
 
+    power = [squared(m) for m in closed]
+    stack = []
+    for c in range(2):
+        double_ref[c] = power[c]
+        gb = times(gain[c], packed(closed[c]))
+        stack.append(jnp.concatenate([gb, gain[c]] if c == 0 else [gain[c], gb], axis=0))
+
+    levels = chunks.bit_length() - 1
+    first_level = CHUNK.bit_length() - 1
+    exponent = 1
+
+    def advance():
+        nonlocal exponent
+        for c in range(2):
+            both = packed(power[c])
+            if exponent < first_level:
+                stack[c] = jnp.concatenate([times(stack[c], both), stack[c]], axis=0)
+            else:
+                powers_ref[c, exponent - first_level] = both
+            if exponent - first_level == levels - 1:
+                last_ref[c] = power[c]
+            else:
+                power[c] = squared(power[c])
+        exponent += 1
+
     large.wait()
     row = lax.broadcasted_iota(jnp.int32, (per_block, LANES), 0)
     wide = lax.broadcasted_iota(jnp.int32, (per_block, LANES), 1)
@@ -130,55 +163,41 @@
             phi_ref[c, b * per_block : (b + 1) * per_block, :] = jnp.broadcast_to(
                 total, (per_block, LANES)
             )
+        if b % 3 == 1:
+            advance()
 
     low_half = lane < obs
+    total = [jnp.zeros((chunks, 2 * LANES), F32) for _ in range(2)]
     for p in range(CHUNK // 2):
         even = yt_ref[pl.ds(2 * p, chunks, stride=PITCH), :]
         odd = pltpu.roll(yt_ref[pl.ds(2 * p + 1, chunks, stride=PITCH), :], obs, 1)
-        pairs_ref[0, p] = side_by_side(jnp.where(low_half, even, odd))
-        pairs_ref[1, p] = side_by_side(jnp.where(low_half, odd, even))
-
-    powers = []
-    for c in range(2):
-        b1, g = closed[c], gain[c]
-        power = squared(b1)
-        double_ref[c] = power
-        gb = times(g, packed(b1))
-        stack = jnp.concatenate([gb, g] if c == 0 else [g, gb], axis=0)
-        reach = 2
-        while reach < CHUNK:
-            stack = jnp.concatenate([times(stack, packed(power)), stack], axis=0)
-            power = squared(power)
-            reach *= 2
-        total = jnp.zeros((chunks, 2 * LANES), F32)
-        for p in range(CHUNK // 2):
-            both = packed(stack[p * LANES : (p + 1) * LANES])
-            total = total + dot(pairs_ref[c, p], jnp.concatenate([both, both], axis=0))
-        powers.append(power)
-        sums_ref[c] = phi_ref[c] * (total[:, :LANES] + total[:, LANES:])
-
-    levels = chunks.bit_length() - 1
+        for c in range(2):
+            value = jnp.where(low_half, even, odd) if c == 0 else jnp.where(low_half, odd, even)
+            pairs_ref[c, p] = side_by_side(value)
+            both = packed(stack[c][p * LANES : (p + 1) * LANES])
+            total[c] = total[c] + dot(pairs_ref[c, p], jnp.concatenate([both, both], axis=0))
+    for c in range(2):
+        sums_ref[c] = phi_ref[c] * (total[c][:, :LANES] + total[c][:, LANES:])
+
     for level in range(levels):
         half = chunks >> (level + 1)
-        for c in range(2):
-            both = packed(powers[c])
-            powers_ref[c, level] = both
-            source, factors = (sums_ref, phi_ref) if level == 0 else (tree_ref, treef_ref)
-            base = 0 if level == 0 else chunks - 4 * half
-            first = source[c, pl.ds(base, half, stride=2), :]
-            second = source[c, pl.ds(base + 1, half, stride=2), :]
-            f0 = factors[c, pl.ds(base, half, stride=2), :]
-            f1 = factors[c, pl.ds(base + 1, half, stride=2), :]
-            state = second + f1 * times(first, both)
-            at = chunks - 2 * half
-            tree_ref[c, at : at + half, :] = state
-            treef_ref[c, at : at + half, :] = f0 * f1
+        rows = max(half, 8)
+        source, factors = (sums_ref, phi_ref) if level == 0 else (tree_ref, treef_ref)
+        base = 0 if level == 0 else chunks - 4 * half
+        at = chunks - 2 * half
+        for c in range(2):
+            first = source[c, pl.ds(base, rows, stride=2), :]
+            second = source[c, pl.ds(base + 1, rows, stride=2), :]
+            f0 = factors[c, pl.ds(base, rows, stride=2), :]
+            f1 = factors[c, pl.ds(base + 1, rows, stride=2), :]
+            state = second + f1 * times_rows(first, powers_ref[c, level])
+            factor = f0 * f1
             if level == levels - 1:
-                last_ref[c] = powers[c]
-                ends_ref[c : c + 1, :] = state
-                ends_ref[2 + c : 3 + c, :] = f0 * f1
+                ends_ref[c : c + 1, :] = state[:1]
+                ends_ref[2 + c : 3 + c, :] = factor[:1]
             else:
-                powers[c] = squared(powers[c])
+                tree_ref[c, at : at + half, :] = state[:half]
+                treef_ref[c, at : at + half, :] = factor[:half]
 
 
 def between(
@@ -257,42 +276,61 @@
     position = lax.axis_index("tm")
     some = [(position >= k).astype(F32) for k in (1, 2, 3)]
 
-    x = []
-    for c in range(2):
-        section = section_ref[c]
-        s = [r[c : c + 1, :] * m for r, m in zip((one_ref, two_ref, three_ref), some)]
-        f = [r[2 + c : 3 + c, :] * m for r, m in zip((one_ref, two_ref, three_ref), some)]
-        wide = lambda v: jnp.broadcast_to(v, (8, LANES))
-        inner = wide(s[1]) + wide(f[1]) * times(wide(s[2]), section)
-        entering = wide(s[0]) + wide(f[0]) * times(inner, section)
-        carry_ref[c, :8, :] = entering
-        for level in range(levels):
-            reach = 1 << level
-            rows = max(reach, 8)
-            moved = times(carry_ref[c, :rows, :], powers_ref[c, level])
-            carry_ref[c, pl.ds(reach, rows), :] = moved
-        pad_ref[0, :8, :] = jnp.zeros((8, LANES), F32)
-        pad_ref[1, :8, :] = jnp.ones((8, LANES), F32)
-        pad_ref[0, 8:, :] = scan_ref[c]
-        pad_ref[1, 8:, :] = cum_ref[c]
-        x.append(
-            pad_ref[0, pl.ds(7, chunks), :]
-            + pad_ref[1, pl.ds(7, chunks), :] * carry_ref[c, :chunks, :]
-        )
+    wide = lambda v: jnp.broadcast_to(v, (8, LANES))
+    arrived = (one_ref, two_ref, three_ref)
+    s = [[wide(r[c : c + 1, :] * m) for r, m in zip(arrived, some)] for c in range(2)]
+    f = [[wide(r[2 + c : 3 + c, :] * m) for r, m in zip(arrived, some)] for c in range(2)]
+    entering = [s[c][2] for c in range(2)]
+    for k in (1, 0):
+        for c in range(2):
+            entering[c] = s[c][k] + f[c][k] * times_rows(entering[c], section_ref[c])
+    for c in range(2):
+        carry_ref[c, :8, :] = entering[c]
+        pad_ref[c, 0, :8, :] = jnp.zeros((8, LANES), F32)
+        pad_ref[c, 1, :8, :] = jnp.ones((8, LANES), F32)
+        pad_ref[c, 0, 8:, :] = scan_ref[c]
+        pad_ref[c, 1, 8:, :] = cum_ref[c]
+    for level in range(levels):
+        reach = 1 << level
+        rows = max(reach, 8)
+        for c in range(2):
+            carry_ref[c, pl.ds(reach, rows), :] = times_rows(
+                carry_ref[c, :rows, :], powers_ref[c, level]
+            )
+    x = [
+        pad_ref[c, 0, pl.ds(7, chunks), :]
+        + pad_ref[c, 1, pl.ds(7, chunks), :] * carry_ref[c, :chunks, :]
+        for c in range(2)
+    ]
 
     row = lax.broadcasted_iota(jnp.int32, (LANES, LANES), 0)
     col = lax.broadcasted_iota(jnp.int32, (LANES, LANES), 1)
     score = [jnp.zeros((chunks, LANES), F32) for _ in range(2)]
     copies = []
+    waiting = [None, None]
+
+    def settle(c):
+        p, seen = waiting[c]
+        innovation = parte_ref[c, p] - (seen[:, :LANES] + seen[:, LANES:])
+        w = weight_ref[c : c + 1, :]
+        term = innovation * innovation * jnp.concatenate([w, w], axis=1)
+        pick = jnp.where(col == 2 * p + row // obs, 1.0, 0.0).astype(BF16)
+        score[c] = score[c] + dot(side_by_side(term), jnp.concatenate([pick, pick], axis=0))
+
     for p in range(CHUNK // 2):
-        for c in range(2):
-            both = side_by_side(x[c])
-            out = partx_ref[c, p] + dot(
-                jnp.concatenate([both, both[:, :LANES]], axis=1), stepx_ref[c]
-            )
-            seen = dot(both, stepe_ref[c])
-            x[c] = out[:, LANES:]
-            xt_ref[c, 2 * p] = out[:, :LANES]
+        both = [side_by_side(x[c]) for c in range(2)]
+        out = [
+            dot(jnp.concatenate([both[c], both[c][:, :LANES]], axis=1), stepx_ref[c])
+            for c in range(2)
+        ]
+        if p:
+            for c in range(2):
+                settle(c)
+        for c in range(2):
+            waiting[c] = p, dot(both[c], stepe_ref[c])
+        for c in range(2):
+            x[c] = partx_ref[c, p, :, LANES:] + out[c][:, LANES:]
+            xt_ref[c, 2 * p] = partx_ref[c, p, :, :LANES] + out[c][:, :LANES]
             xt_ref[c, 2 * p + 1] = x[c]
             pair = pl.ds(2 * p, 2)
             copy = pltpu.make_async_copy(
@@ -300,11 +338,8 @@
             )
             copy.start()
             copies.append(copy)
-            innovation = parte_ref[c, p] - (seen[:, :LANES] + seen[:, LANES:])
-            w = weight_ref[c : c + 1, :]
-            term = innovation * innovation * jnp.concatenate([w, w], axis=1)
-            pick = jnp.where(col == 2 * p + row // obs, 1.0, 0.0).astype(BF16)
-            score[c] = score[c] + dot(side_by_side(term), jnp.concatenate([pick, pick], axis=0))
+    for c in range(2):
+        settle(c)
 
     total = score[0] * square_ref[0] + score[1] * square_ref[1]
     lanes = lax.broadcasted_iota(jnp.int32, (1, LANES), 1)
@@ -314,7 +349,8 @@
         jnp.ones((8, LANES), F32), per_batch, (((1,), (1,)), ((), ())),
         precision=HIGHEST, preferred_element_type=F32,
     )
-    nis_ref[...] = jnp.broadcast_to(local[:1][None], nis_ref.shape)
+    divisor = 2 * nis_ref.shape[0] * BATCH * obs
+    nis_ref[...] = jnp.broadcast_to((local[:1] / divisor)[None], nis_ref.shape)
     for copy in copies:
         copy.wait()
 
@@ -382,8 +418,8 @@
         scratch_shapes=[
             pltpu.VMEM((chunks * PITCH, LANES), F32),
             pltpu.VMEM((2 * blocks, LANES), F32),
-            pltpu.VMEM((channels, chunks, width), F32),
-            pltpu.VMEM((channels, chunks, width), F32),
+            pltpu.VMEM((channels, chunks + 16, width), F32),
+            pltpu.VMEM((channels, chunks + 16, width), F32),
             pltpu.VMEM((channels * obs, frames), F32),
             pltpu.VMEM(fading.shape, F32),
             pltpu.VMEM(transition.shape, F32),
@@ -445,7 +481,7 @@
         out_specs=[pl.BlockSpec(memory_space=pltpu.HBM), vmem],
         scratch_shapes=[
             pltpu.VMEM((channels, chunks + 8, width), F32),
-            pltpu.VMEM((2, chunks + 8, width), F32),
+            pltpu.VMEM((channels, 2, chunks + 8, width), F32),
             pltpu.VMEM((channels, CHUNK, chunks, width), F32),
             pltpu.SemaphoreType.DMA((channels, CHUNK // 2)),
         ],
@@ -473,8 +509,7 @@
         ),
         name="write",
     )(pltpu.with_memory_space_constraint(rows, pltpu.HBM), fade)
-    divisor = channels * lax.axis_size("chan") * BATCH * obs
-    return states, jnp.sum(everything, axis=(0, 1)) / divisor
+    return states, jnp.sum(everything, axis=(0, 1))
 
 
 def solution(mesh):

time: 44.7 us -> 43.1 us (0.964)
  Pallas kernels: 20.1 us -> 18.6 us
    pallas_call x1, Pallas kernels: 6.23 us -> 4.94 us  [per_device(): pl.pallas_call(after, out_shape=[pltpu.HBM((channels, CHUNK, chunks, widt...]
    div x1 -> x0, other arithmetic: 0.52 us -> none  [per_device(): return (states, jnp.sum(everything, axis=(0, 1)) / divisor)]
    reduce_sum x1, other arithmetic: 0.08 us -> 0.59 us  [per_device(): return (states, jnp.sum(everything, axis=(0, 1)))]
where the time goes in v1:
time: 43.1 us; the launch traced here: 43 us
  Pallas kernels  18.6 us (43%)
  starting transfers between devices  18.4 us (43%)
  waiting for transfers between devices  4.65 us (11%)
  between operations  0.7 us (2%)
  other arithmetic  0.59 us (1%)
    all_to_all x1, starting transfers between devices, per_device(): lax.all_to_all(nis, 'chan', split_axis=0, concat_axis=0, tiled=True)  13.9 us
    pallas_call x1, Pallas kernels, per_device(): pl.pallas_call(before, out_shape=first, in_specs=[pl.BlockSpec(memory_spa...  5.79 us
    pallas_call x1, Pallas kernels, per_device(): pl.pallas_call(after, out_shape=[pltpu.HBM((channels, CHUNK, chunks, widt...  4.94 us
    pallas_call x1, Pallas kernels, per_device(): pl.pallas_call(write, out_shape=jax.ShapeDtypeStruct((channels, width, fr...  4.76 us
    all_to_all x1, waiting for transfers between devices, per_device(): lax.all_to_all(nis, 'chan', split_axis=0, concat_axis=0, tiled=True)  4.64 us
    ppermute x3, starting transfers between devices, per_device(): lax.ppermute(ends, 'tm', [(i, (i + s) % sections) for i in range(sections)])  4.49 us
    pallas_call x1, Pallas kernels, per_device(): pl.pallas_call(between, out_shape=second, in_specs=[vmem] * len(kept), ou...  3.1 us
  transfers between devices with their start and end apart: 4, of which 1 were waited for; matrix products, arithmetic and copies ran while one was open for 0% of the time, Pallas kernels for 18%

profile of v1, /device:TPU:1, one launch (start us, length us, event | category | flops | bytes accessed | tf_op | source)
XLA Modules:
  0.0 43.0 jit_solution(11079484288055931591)
XLA Ops:
  0.6 5.8 %before.1 = (f32[4,128]{1,0:T(4,128)S(1)}, f32[2,256,128]{2,1,0:T(8,128)S(1)}, f32[2,256,128]{2,1,0:T(8,128)S(1)}, bf16[2,8,256,256]{3,2,1,0:T(8,128)(2,1)S(1)},...) custom-call(f32[128,4096]{1,0:T(8,128)} %bitcast.1, ...), custom_call_target="tpu_custom_call" | custom-call | tf_op jit(solution)/shard_map/before/pallas_call | solution.py:413
  6.4 3.4 %collective-permute-start.2 = (f32[4,128]{1,0:T(4,128)S(1)}, f32[4,128]{1,0:T(4,128)S(1)}, u32[]{:S(2)}, u32[]{:S(2)}) collective-permute-start(f32[4,128]{1,0:T(4,128)S(1)} %get-tuple-element.23), channel_id=1, source_target_pairs={{0,192},{64,0},{128,64},{192,128},{1,193},{65,1},{129,65},{193,129... | collective-permute-start | bytes 6152 | tf_op jit(solution)/shard_map/ppermute | solution.py:470
  9.8 0.5 %collective-permute-start.1 = (f32[4,128]{1,0:T(4,128)S(1)}, f32[4,128]{1,0:T(4,128)S(1)}, u32[]{:S(2)}, u32[]{:S(2)}) collective-permute-start(f32[4,128]{1,0:T(4,128)S(1)} %get-tuple-element.23), channel_id=1, source_target_pairs={{0,128},{64,192},{128,0},{192,64},{1,129},{65,193},{129,1},{193,65... | collective-permute-start | bytes 6152 | tf_op jit(solution)/shard_map/ppermute | solution.py:470
  10.3 0.6 %collective-permute-start = (f32[4,128]{1,0:T(4,128)S(1)}, f32[4,128]{1,0:T(4,128)S(1)}, u32[]{:S(2)}, u32[]{:S(2)}) collective-permute-start(f32[4,128]{1,0:T(4,128)S(1)} %get-tuple-element.23), channel_id=1, source_target_pairs={{0,64},{64,128},{128,192},{192,0},{1,65},{65,129},{129,193},{193,1... | collective-permute-start | bytes 6152 | tf_op jit(solution)/shard_map/ppermute | solution.py:470
  10.9 0.0 copy-start
  10.9 3.1 %between.1 = (f32[2,256,128]{2,1,0:T(8,128)S(1)}, f32[2,256,128]{2,1,0:T(8,128)S(1)}, f32[2,256,128]{2,1,0:T(8,128)S(1)}, bf16[2,128,256]{2,1,0:T(8,128)(2,1)S(1...) custom-call(f32[2,256,128]{2,1,0:T(8,128)S(1)} %get-tuple-element.24, ...), custom_call_target="tpu_custom_call" | custom-call | flops 4000000000 | bytes 8000000 | tf_op jit(solution)/shard_map/between/pallas_call | solution.py:452
  14.0 0.0 collective-permute-done.2.three_ref
  14.0 0.0 collective-permute-done.1.two_ref
  14.1 0.0 collective-permute-done.one_ref
  14.1 0.0 copy-done
  14.1 4.9 %after.1 = (f32[2,16,256,128]{3,2,1,0:T(8,128)}, f32[64,1,32]{2,1,0:T(1,128)}) custom-call(f32[4,128]{1,0:T(4,128)S(1)} %collective-permute-done.one_ref, f32[4,128]{1,0:T(4,128)S(1)} %collective-permute-done.1.two_ref, f32[4,128]{1,0:T(4,128)S(1)} %collective-permute-done.2.three_ref, f32[2,256,128]{2,1,0:T(8,128)S(1)} %get-tuple-element.34.scan_ref, ...), custom_call_target="tpu_custom_call" | custom-call | flops 4000000000 | bytes 8000000 | tf_op jit(solution)/shard_map/after/pallas_call | solution.py:474
  19.0 13.9 %all-to-all-start = ((f32[64,1,32]{2,1,0:T(1,128)}), f32[64,1,32]{2,1,0:T(1,128)S(1)}, u32[]{:S(2)}, u32[]{:S(2)}) async-start(f32[64,1,32]{2,1,0:T(1,128)} %get-tuple-element.43), calls=%async_computation | async-start | bytes 65536 | tf_op jit(solution)/shard_map/all_to_all | solution.py:494
  33.0 4.8 %write.1 = f32[2,128,4096]{2,1,0:T(8,128)} custom-call(f32[2,16,256,128]{3,2,1,0:T(8,128)} %get-tuple-element.42.rows_ref, f32[64,128]{1,0:T(8,128)S(1)} %get-tuple-element.27.fade_ref), custom_call_target="tpu_custom_call" | custom-call | flops 4000000000 | bytes 8388608 | tf_op jit(solution)/shard_map/write/pallas_call | solution.py:495
  37.7 4.6 %all-to-all-done = f32[64,1,32]{2,1,0:T(1,128)S(1)} async-done(((f32[64,1,32]{2,1,0:T(1,128)}), f32[64,1,32]{2,1,0:T(1,128)S(1)}, u32[]{:S(2)}, u32[]{:S(2)}) %all-to-all-start) | async-done | bytes 8224 | tf_op jit(solution)/shard_map/all_to_all | solution.py:494
  42.4 0.6 %reduce_sum.9 = f32[32]{0:T(128)} reduce(f32[64,1,32]{2,1,0:T(1,128)S(1)} %all-to-all-done, f32[]{:T(128)} %constant.0.clone.1), dimensions={0,1}, to_apply=%region_0.0 | reduce | flops 2016 | bytes 8324 | tf_op jit(solution)/shard_map/reduce_sum | solution.py:512
Async XLA Ops:
  6.4 7.6 %collective-permute-start.2 = (f32[4,128]{1,0:T(4,128)S(1)}, f32[4,128]{1,0:T(4,128)S(1)}, u32[]{:S(2)}, u32[]{:S(2)}) collective-permute-start(f32[4,128]{1,0:T(4,128)S(1)} %get-tuple-element.23), channel_id=1, source_target_pairs={{0,192},{64,0},{128,64},{192,128},{1,193},{65,1},{129,65},{193,129... | collective-permute-start | bytes 6152 | tf_op jit(solution)/shard_map/ppermute | solution.py:470
  9.8 4.2 %collective-permute-start.1 = (f32[4,128]{1,0:T(4,128)S(1)}, f32[4,128]{1,0:T(4,128)S(1)}, u32[]{:S(2)}, u32[]{:S(2)}) collective-permute-start(f32[4,128]{1,0:T(4,128)S(1)} %get-tuple-element.23), channel_id=1, source_target_pairs={{0,128},{64,192},{128,0},{192,64},{1,129},{65,193},{129,1},{193,65... | collective-permute-start | bytes 6152 | tf_op jit(solution)/shard_map/ppermute | solution.py:470
  10.3 3.8 %collective-permute-start = (f32[4,128]{1,0:T(4,128)S(1)}, f32[4,128]{1,0:T(4,128)S(1)}, u32[]{:S(2)}, u32[]{:S(2)}) collective-permute-start(f32[4,128]{1,0:T(4,128)S(1)} %get-tuple-element.23), channel_id=1, source_target_pairs={{0,64},{64,128},{128,192},{192,0},{1,65},{65,129},{129,193},{193,1... | collective-permute-start | bytes 6152 | tf_op jit(solution)/shard_map/ppermute | solution.py:470
  10.9 3.1 %copy-start = (f32[2,64]{1,0:T(2,128)S(1)}, f32[2,64]{1,0:T(2,128)}, u32[]{:S(2)}) copy-start(f32[2,64]{1,0:T(2,128)} %weight_ref.1) | copy-start | bytes 1540
  19.0 23.4 %all-to-all-start = ((f32[64,1,32]{2,1,0:T(1,128)}), f32[64,1,32]{2,1,0:T(1,128)S(1)}, u32[]{:S(2)}, u32[]{:S(2)}) async-start(f32[64,1,32]{2,1,0:T(1,128)} %get-tuple-element.43), calls=%async_computation | async-start | bytes 65536 | tf_op jit(solution)/shard_map/all_to_all | solution.py:494

commit v2 on v1

--- a/solution.py
+++ b/solution.py
@@ -61,9 +61,16 @@
 
 
 def times_rows(x, both):
-    rows = x.shape[0]
+    return folded(dot(stacked(x), both))
+
+
+def stacked(x):
     high = x.astype(BF16).astype(F32)
-    out = dot(jnp.concatenate([high, x - high], axis=0).astype(BF16), both)
+    return jnp.concatenate([high, x - high], axis=0).astype(BF16)
+
+
+def folded(out):
+    rows = out.shape[0] // 2
     out = out[:rows] + out[rows:]
     return out[:, :LANES] + out[:, LANES:]
 
@@ -71,7 +78,7 @@
 def before(
     y_hbm, f_hbm, t_hbm, h_hbm, w_hbm,
     ends_ref, sums_ref, phi_ref, pairs_ref, fade_ref, powers_ref, last_ref, closed_ref, double_ref,
-    gain_ref, seen_ref,
+    gain_ref, seen_ref, triple_ref,
     yt_ref, inv_ref, tree_ref, treef_ref, y_ref, f_ref, t_ref, h_ref, w_ref, in_sem,
 ):
     small = [
@@ -103,33 +110,52 @@
     fade_ref[...] = run
     inv_ref[...] = 1.0 / run
 
-    closed, gain = [], []
-    for c in range(2):
-        t, h = t_ref[c], h_ref[c]
-        eye = lax.broadcasted_iota(jnp.int32, (obs, obs), 0) == lax.broadcasted_iota(
-            jnp.int32, (obs, obs), 1
-        )
-        column = jnp.sum(jnp.where(eye, w_ref[c : c + 1, :], 0.0), axis=1, keepdims=True)
-        g = column * h
-        q = lax.dot_general(
-            t, h, (((1,), (1,)), ((), ())), precision=HIGHEST, preferred_element_type=F32
-        )
-        closed.append(t - exact_dot(q, g))
-        gain.append(g)
-        closed_ref[c] = closed[c]
-        gain_ref[c] = g
-        seen_ref[c] = q
-
-    power = [squared(m) for m in closed]
-    stack = []
-    for c in range(2):
-        double_ref[c] = power[c]
-        gb = times(gain[c], packed(closed[c]))
-        stack.append(jnp.concatenate([gb, gain[c]] if c == 0 else [gain[c], gb], axis=0))
+    half_lane = lane < obs
+    closed, gain, seen = [None, None], [None, None], [None, None]
+
+    def first_step():
+        for c in range(2):
+            t, h = t_ref[c], h_ref[c]
+            eye = lax.broadcasted_iota(jnp.int32, (obs, obs), 0) == lax.broadcasted_iota(
+                jnp.int32, (obs, obs), 1
+            )
+            column = jnp.sum(jnp.where(eye, w_ref[c : c + 1, :], 0.0), axis=1, keepdims=True)
+            gain[c] = column * h
+            gain_ref[c] = gain[c]
+            t1, t2, t3 = thirds(t)
+            h1, h2, h3 = thirds(jnp.concatenate([h, h], axis=0))
+            seen[c] = lax.dot_general(
+                jnp.concatenate([t1, t1, t1, t2, t2, t3], axis=1),
+                jnp.concatenate([h1, h2, h3, h1, h2, h1], axis=1),
+                (((1,), (1,)), ((), ())),
+                preferred_element_type=F32,
+            )
+            seen_ref[c] = seen[c][:, :obs]
+
+    def second_step():
+        for c in range(2):
+            q1, q2, q3 = (v.astype(F32) for v in thirds(seen[c]))
+            mixed = jnp.where(half_lane, q1, q3)
+            g1, g2, g3 = thirds(gain[c])
+            closed[c] = t_ref[c] - dot(
+                jnp.concatenate([q1, q2, mixed], axis=1).astype(BF16),
+                jnp.concatenate([g1, g2, g1, g2, g3, g1], axis=0),
+            )
+            closed_ref[c] = closed[c]
+
+    power, stack = [None, None], [None, None]
+
+    def third_step():
+        for c in range(2):
+            power[c] = squared(closed[c])
+            double_ref[c] = power[c]
+            gb = times(gain[c], packed(closed[c]))
+            stack[c] = jnp.concatenate([gb, gain[c]] if c == 0 else [gain[c], gb], axis=0)
 
     levels = chunks.bit_length() - 1
     first_level = CHUNK.bit_length() - 1
     exponent = 1
+    below = [None, None]
 
     def advance():
         nonlocal exponent
@@ -138,14 +164,22 @@
             if exponent < first_level:
                 stack[c] = jnp.concatenate([times(stack[c], both), stack[c]], axis=0)
             else:
-                powers_ref[c, exponent - first_level] = both
+                level = exponent - first_level
+                powers_ref[c, level] = both
+                if level % 2:
+                    triple_ref[c, level // 2] = packed(times(below[c], both))
+                below[c] = power[c]
             if exponent - first_level == levels - 1:
                 last_ref[c] = power[c]
             else:
                 power[c] = squared(power[c])
         exponent += 1
 
+    first_step()
+    second_step()
+    third_step()
     large.wait()
+    steps = [advance] * (levels + first_level - 1)
     row = lax.broadcasted_iota(jnp.int32, (per_block, LANES), 0)
     wide = lax.broadcasted_iota(jnp.int32, (per_block, LANES), 1)
     last = wide == row * CHUNK + (CHUNK - 1)
@@ -163,8 +197,11 @@
             phi_ref[c, b * per_block : (b + 1) * per_block, :] = jnp.broadcast_to(
                 total, (per_block, LANES)
             )
-        if b % 3 == 1:
-            advance()
+        if b % 3 == 1 and steps:
+            steps.pop(0)()
+
+    for step in steps:
+        step()
 
     low_half = lane < obs
     total = [jnp.zeros((chunks, 2 * LANES), F32) for _ in range(2)]
@@ -179,25 +216,30 @@
     for c in range(2):
         sums_ref[c] = phi_ref[c] * (total[c][:, :LANES] + total[c][:, LANES:])
 
-    for level in range(levels):
-        half = chunks >> (level + 1)
-        rows = max(half, 8)
-        source, factors = (sums_ref, phi_ref) if level == 0 else (tree_ref, treef_ref)
-        base = 0 if level == 0 else chunks - 4 * half
-        at = chunks - 2 * half
-        for c in range(2):
-            first = source[c, pl.ds(base, rows, stride=2), :]
-            second = source[c, pl.ds(base + 1, rows, stride=2), :]
-            f0 = factors[c, pl.ds(base, rows, stride=2), :]
-            f1 = factors[c, pl.ds(base + 1, rows, stride=2), :]
-            state = second + f1 * times_rows(first, powers_ref[c, level])
-            factor = f0 * f1
-            if level == levels - 1:
+    source, factors, base, at = sums_ref, phi_ref, 0, 0
+    for level in range(levels // 2):
+        count = chunks >> (2 * level + 2)
+        rows = max(count, 8)
+        for c in range(2):
+            e = [source[c, pl.ds(base + k, rows, stride=4), :] for k in range(4)]
+            f = [factors[c, pl.ds(base + k, rows, stride=4), :] for k in range(4)]
+            f2 = f[3] * f[2]
+            f1 = f2 * f[1]
+            weights = jnp.concatenate(
+                [powers_ref[c, 2 * level], powers_ref[c, 2 * level + 1], triple_ref[c, level]],
+                axis=0,
+            )
+            moved = jnp.concatenate([e[2] * f[3], e[1] * f2, e[0] * f1], axis=1)
+            state = e[3] + folded(dot(stacked(moved), weights))
+            factor = f1 * f[0]
+            if level == levels // 2 - 1:
                 ends_ref[c : c + 1, :] = state[:1]
                 ends_ref[2 + c : 3 + c, :] = factor[:1]
             else:
-                tree_ref[c, at : at + half, :] = state[:half]
-                treef_ref[c, at : at + half, :] = factor[:half]
+                tree_ref[c, at : at + count, :] = state[:count]
+                treef_ref[c, at : at + count, :] = factor[:count]
+        source, factors, base = tree_ref, treef_ref, at
+        at += count
 
 
 def between(
@@ -222,7 +264,8 @@
 
     weights = []
     for c in range(2):
-        section_ref[c] = packed(squared(last_ref[c]))
+        section = squared(last_ref[c])
+        section_ref[c] = jnp.concatenate([packed(section), packed(squared(section))], axis=0)
         b1, b2, g, q = closed_ref[c], double_ref[c], gain_ref[c], seen_ref[c]
         gb, bq, gq = exact_dot(g, b1), exact_dot(b1, q), exact_dot(g, q)
         high, low = halves(jnp.concatenate([b1, b2], axis=1))
@@ -264,7 +307,7 @@
 
 def after(
     one_ref, two_ref, three_ref, scan_ref, cum_ref, square_ref, section_ref, stepx_ref, stepe_ref,
-    partx_ref, parte_ref, powers_ref, weight_ref,
+    partx_ref, parte_ref, powers_ref, triple_ref, weight_ref,
     rows_ref, nis_ref,
     carry_ref, pad_ref, xt_ref, sem,
 ):
@@ -280,23 +323,25 @@
     arrived = (one_ref, two_ref, three_ref)
     s = [[wide(r[c : c + 1, :] * m) for r, m in zip(arrived, some)] for c in range(2)]
     f = [[wide(r[2 + c : 3 + c, :] * m) for r, m in zip(arrived, some)] for c in range(2)]
-    entering = [s[c][2] for c in range(2)]
-    for k in (1, 0):
-        for c in range(2):
-            entering[c] = s[c][k] + f[c][k] * times_rows(entering[c], section_ref[c])
+    entering = []
+    for c in range(2):
+        earlier = jnp.concatenate([f[c][0] * s[c][1], f[c][0] * f[c][1] * s[c][2]], axis=1)
+        entering.append(s[c][0] + folded(dot(stacked(earlier), section_ref[c])))
     for c in range(2):
         carry_ref[c, :8, :] = entering[c]
         pad_ref[c, 0, :8, :] = jnp.zeros((8, LANES), F32)
         pad_ref[c, 1, :8, :] = jnp.ones((8, LANES), F32)
         pad_ref[c, 0, 8:, :] = scan_ref[c]
         pad_ref[c, 1, 8:, :] = cum_ref[c]
-    for level in range(levels):
-        reach = 1 << level
+    for level in range(levels // 2):
+        reach = 1 << (2 * level)
         rows = max(reach, 8)
         for c in range(2):
-            carry_ref[c, pl.ds(reach, rows), :] = times_rows(
-                carry_ref[c, :rows, :], powers_ref[c, level]
-            )
+            few = stacked(carry_ref[c, :rows, :])
+            weights = (powers_ref[c, 2 * level], powers_ref[c, 2 * level + 1], triple_ref[c, level])
+            moved = [folded(dot(few, m)) for m in weights]
+            for k in range(3):
+                carry_ref[c, pl.ds((k + 1) * reach, rows), :] = moved[k]
     x = [
         pad_ref[c, 0, pl.ds(7, chunks), :]
         + pad_ref[c, 1, pl.ds(7, chunks), :] * carry_ref[c, :chunks, :]
@@ -346,8 +391,8 @@
     total = jnp.where(lanes < CHUNK, total, 0.0)
     per_batch = jnp.sum(total.reshape(blocks, per_block, LANES), axis=1)
     local = lax.dot_general(
-        jnp.ones((8, LANES), F32), per_batch, (((1,), (1,)), ((), ())),
-        precision=HIGHEST, preferred_element_type=F32,
+        jnp.ones((8, 3 * LANES), BF16), jnp.concatenate(thirds(per_batch), axis=1),
+        (((1,), (1,)), ((), ())), preferred_element_type=F32,
     )
     divisor = 2 * nis_ref.shape[0] * BATCH * obs
     nis_ref[...] = jnp.broadcast_to((local[:1] / divisor)[None], nis_ref.shape)
@@ -409,8 +454,9 @@
         spec((channels, width, width), F32),
         spec((channels, obs, width), F32),
         spec((channels, width, obs), F32),
+        spec((channels, levels // 2, width, 2 * width), BF16),
     ]
-    ends, *kept = pl.pallas_call(
+    ends, *kept, triples = pl.pallas_call(
         before,
         out_shape=first,
         in_specs=[pl.BlockSpec(memory_space=pltpu.HBM)] * 5,
@@ -443,7 +489,7 @@
         spec((channels, chunks, width), F32),
         spec((channels, chunks, width), F32),
         spec((channels, chunks, LANES), F32),
-        spec((channels, width, 2 * width), BF16),
+        spec((channels, 2 * width, 2 * width), BF16),
         spec((channels, 3 * width, 2 * width), BF16),
         spec((channels, 2 * width, 4 * obs), BF16),
         spec((channels, CHUNK // 2, chunks, 2 * width), F32),
@@ -477,7 +523,7 @@
             pltpu.HBM((channels, CHUNK, chunks, width), F32),
             spec((group, 1, blocks), F32),
         ],
-        in_specs=[vmem] * (5 + len(second)),
+        in_specs=[vmem] * (6 + len(second)),
         out_specs=[pl.BlockSpec(memory_space=pltpu.HBM), vmem],
         scratch_shapes=[
             pltpu.VMEM((channels, chunks + 8, width), F32),
@@ -490,7 +536,7 @@
             flops=4_000_000_000, bytes_accessed=8_000_000, transcendentals=0
         ),
         name="after",
-    )(*arrived, *made, powers, obs_precision)
+    )(*arrived, *made, powers, triples, obs_precision)
     everything = lax.all_to_all(nis, "chan", split_axis=0, concat_axis=0, tiled=True)
     states = pl.pallas_call(
         write,

time: 43.1 us -> 42.3 us (0.981)
  Pallas kernels: 18.6 us -> 18.1 us
    pallas_call x1, Pallas kernels: 4.94 us -> 4.37 us  [per_device(): pl.pallas_call(after, out_shape=[pltpu.HBM((channels, CHUNK, chunks, widt...]
  transfers between devices with their start and end apart: 4 -> 4, of which waited for: 1 -> 1; matrix products, arithmetic and copies ran while one was open for 0% -> 0% of each run, Pallas kernels for 18% -> 19%
where the time goes in v2:
time: 42.3 us; the launch traced here: 42.1 us
  Pallas kernels  18.1 us (43%)
  starting transfers between devices  18.1 us (43%)
  waiting for transfers between devices  4.65 us (11%)
  between operations  0.71 us (2%)
  other arithmetic  0.59 us (1%)
    all_to_all x1, starting transfers between devices, per_device(): lax.all_to_all(nis, 'chan', split_axis=0, concat_axis=0, tiled=True)  13.6 us
    pallas_call x1, Pallas kernels, per_device(): pl.pallas_call(before, out_shape=first, in_specs=[pl.BlockSpec(memory_spa...  5.49 us
    pallas_call x1, Pallas kernels, per_device(): pl.pallas_call(write, out_shape=jax.ShapeDtypeStruct((channels, width, fr...  4.76 us
    all_to_all x1, waiting for transfers between devices, per_device(): lax.all_to_all(nis, 'chan', split_axis=0, concat_axis=0, tiled=True)  4.64 us
    ppermute x3, starting transfers between devices, per_device(): lax.ppermute(ends, 'tm', [(i, (i + s) % sections) for i in range(sections)])  4.5 us
    pallas_call x1, Pallas kernels, per_device(): pl.pallas_call(after, out_shape=[pltpu.HBM((channels, CHUNK, chunks, widt...  4.37 us
    pallas_call x1, Pallas kernels, per_device(): pl.pallas_call(between, out_shape=second, in_specs=[vmem] * len(kept), ou...  3.43 us
  transfers between devices with their start and end apart: 4, of which 1 were waited for; matrix products, arithmetic and copies ran while one was open for 0% of the time, Pallas kernels for 19%

profile of v2, /device:TPU:1, one launch (start us, length us, event | category | flops | bytes accessed | tf_op | source)
XLA Modules:
  0.0 42.1 jit_solution(15493519756103352526)
XLA Ops:
  0.6 5.5 %before.1 = (f32[4,128]{1,0:T(4,128)S(1)}, f32[2,256,128]{2,1,0:T(8,128)S(1)}, f32[2,256,128]{2,1,0:T(8,128)S(1)}, bf16[2,8,256,256]{3,2,1,0:T(8,128)(2,1)S(1)},...) custom-call(f32[128,4096]{1,0:T(8,128)} %bitcast.1, ...), custom_call_target="tpu_custom_call" | custom-call | tf_op jit(solution)/shard_map/before/pallas_call | solution.py:459
  6.1 3.4 %collective-permute-start.2 = (f32[4,128]{1,0:T(4,128)S(1)}, f32[4,128]{1,0:T(4,128)S(1)}, u32[]{:S(2)}, u32[]{:S(2)}) collective-permute-start(f32[4,128]{1,0:T(4,128)S(1)} %get-tuple-element.24), channel_id=1, source_target_pairs={{0,192},{64,0},{128,64},{192,128},{1,193},{65,1},{129,65},{193,129... | collective-permute-start | bytes 6152 | tf_op jit(solution)/shard_map/ppermute | solution.py:516
  9.5 0.5 %collective-permute-start.1 = (f32[4,128]{1,0:T(4,128)S(1)}, f32[4,128]{1,0:T(4,128)S(1)}, u32[]{:S(2)}, u32[]{:S(2)}) collective-permute-start(f32[4,128]{1,0:T(4,128)S(1)} %get-tuple-element.24), channel_id=1, source_target_pairs={{0,128},{64,192},{128,0},{192,64},{1,129},{65,193},{129,1},{193,65... | collective-permute-start | bytes 6152 | tf_op jit(solution)/shard_map/ppermute | solution.py:516
  10.0 0.6 %collective-permute-start = (f32[4,128]{1,0:T(4,128)S(1)}, f32[4,128]{1,0:T(4,128)S(1)}, u32[]{:S(2)}, u32[]{:S(2)}) collective-permute-start(f32[4,128]{1,0:T(4,128)S(1)} %get-tuple-element.24), channel_id=1, source_target_pairs={{0,64},{64,128},{128,192},{192,0},{1,65},{65,129},{129,193},{193,1... | collective-permute-start | bytes 6152 | tf_op jit(solution)/shard_map/ppermute | solution.py:516
  10.6 0.0 copy-start
  10.6 3.4 %between.1 = (f32[2,256,128]{2,1,0:T(8,128)S(1)}, f32[2,256,128]{2,1,0:T(8,128)S(1)}, f32[2,256,128]{2,1,0:T(8,128)S(1)}, bf16[2,256,256]{2,1,0:T(8,128)(2,1)S(1...) custom-call(f32[2,256,128]{2,1,0:T(8,128)S(1)} %get-tuple-element.25, ...), custom_call_target="tpu_custom_call" | custom-call | flops 4000000000 | bytes 8000000 | tf_op jit(solution)/shard_map/between/pallas_call | solution.py:498
  14.1 0.0 collective-permute-done.2.three_ref
  14.1 0.0 collective-permute-done.1.two_ref
  14.1 0.0 collective-permute-done.one_ref
  14.1 0.0 copy-done
  14.1 4.4 %after.1 = (f32[2,16,256,128]{3,2,1,0:T(8,128)}, f32[64,1,32]{2,1,0:T(1,128)}) custom-call(f32[4,128]{1,0:T(4,128)S(1)} %collective-permute-done.one_ref, f32[4,128]{1,0:T(4,128)S(1)} %collective-permute-done.1.two_ref, f32[4,128]{1,0:T(4,128)S(1)} %collective-permute-done.2.three_ref, f32[2,256,128]{2,1,0:T(8,128)S(1)} %get-tuple-element.35.scan_ref, ...), custom_call_target="tpu_custom_call" | custom-call | flops 4000000000 | bytes 8000000 | tf_op jit(solution)/shard_map/after/pallas_call | solution.py:520
  18.5 13.6 %all-to-all-start = ((f32[64,1,32]{2,1,0:T(1,128)}), f32[64,1,32]{2,1,0:T(1,128)S(1)}, u32[]{:S(2)}, u32[]{:S(2)}) async-start(f32[64,1,32]{2,1,0:T(1,128)} %get-tuple-element.45), calls=%async_computation | async-start | bytes 65536 | tf_op jit(solution)/shard_map/all_to_all | solution.py:540
  32.1 4.8 %write.1 = f32[2,128,4096]{2,1,0:T(8,128)} custom-call(f32[2,16,256,128]{3,2,1,0:T(8,128)} %get-tuple-element.44.rows_ref, f32[64,128]{1,0:T(8,128)S(1)} %get-tuple-element.28.fade_ref), custom_call_target="tpu_custom_call" | custom-call | flops 4000000000 | bytes 8388608 | tf_op jit(solution)/shard_map/write/pallas_call | solution.py:541
  36.9 4.6 %all-to-all-done = f32[64,1,32]{2,1,0:T(1,128)S(1)} async-done(((f32[64,1,32]{2,1,0:T(1,128)}), f32[64,1,32]{2,1,0:T(1,128)S(1)}, u32[]{:S(2)}, u32[]{:S(2)}) %all-to-all-start) | async-done | bytes 8224 | tf_op jit(solution)/shard_map/all_to_all | solution.py:540
  41.5 0.6 %reduce_sum.9 = f32[32]{0:T(128)} reduce(f32[64,1,32]{2,1,0:T(1,128)S(1)} %all-to-all-done, f32[]{:T(128)} %constant.0.clone.1), dimensions={0,1}, to_apply=%region_0.0 | reduce | flops 2016 | bytes 8324 | tf_op jit(solution)/shard_map/reduce_sum | solution.py:558
Async XLA Ops:
  6.1 7.9 %collective-permute-start.2 = (f32[4,128]{1,0:T(4,128)S(1)}, f32[4,128]{1,0:T(4,128)S(1)}, u32[]{:S(2)}, u32[]{:S(2)}) collective-permute-start(f32[4,128]{1,0:T(4,128)S(1)} %get-tuple-element.24), channel_id=1, source_target_pairs={{0,192},{64,0},{128,64},{192,128},{1,193},{65,1},{129,65},{193,129... | collective-permute-start | bytes 6152 | tf_op jit(solution)/shard_map/ppermute | solution.py:516
  9.5 4.6 %collective-permute-start.1 = (f32[4,128]{1,0:T(4,128)S(1)}, f32[4,128]{1,0:T(4,128)S(1)}, u32[]{:S(2)}, u32[]{:S(2)}) collective-permute-start(f32[4,128]{1,0:T(4,128)S(1)} %get-tuple-element.24), channel_id=1, source_target_pairs={{0,128},{64,192},{128,0},{192,64},{1,129},{65,193},{129,1},{193,65... | collective-permute-start | bytes 6152 | tf_op jit(solution)/shard_map/ppermute | solution.py:516
  10.0 4.1 %collective-permute-start = (f32[4,128]{1,0:T(4,128)S(1)}, f32[4,128]{1,0:T(4,128)S(1)}, u32[]{:S(2)}, u32[]{:S(2)}) collective-permute-start(f32[4,128]{1,0:T(4,128)S(1)} %get-tuple-element.24), channel_id=1, source_target_pairs={{0,64},{64,128},{128,192},{192,0},{1,65},{65,129},{129,193},{193,1... | collective-permute-start | bytes 6152 | tf_op jit(solution)/shard_map/ppermute | solution.py:516
  10.6 3.5 %copy-start = (f32[2,64]{1,0:T(2,128)S(1)}, f32[2,64]{1,0:T(2,128)}, u32[]{:S(2)}) copy-start(f32[2,64]{1,0:T(2,128)} %weight_ref.1) | copy-start | bytes 1540
  18.5 23.0 %all-to-all-start = ((f32[64,1,32]{2,1,0:T(1,128)}), f32[64,1,32]{2,1,0:T(1,128)S(1)}, u32[]{:S(2)}, u32[]{:S(2)}) async-start(f32[64,1,32]{2,1,0:T(1,128)} %get-tuple-element.45), calls=%async_computation | async-start | bytes 65536 | tf_op jit(solution)/shard_map/all_to_all | solution.py:540

commit v3 on v2

--- a/solution.py
+++ b/solution.py
@@ -348,8 +348,7 @@
         for c in range(2)
     ]
 
-    row = lax.broadcasted_iota(jnp.int32, (LANES, LANES), 0)
-    col = lax.broadcasted_iota(jnp.int32, (LANES, LANES), 1)
+    first_half = lax.broadcasted_iota(jnp.int32, (1, LANES), 1) < obs
     score = [jnp.zeros((chunks, LANES), F32) for _ in range(2)]
     copies = []
     waiting = [None, None]
@@ -359,8 +358,8 @@
         innovation = parte_ref[c, p] - (seen[:, :LANES] + seen[:, LANES:])
         w = weight_ref[c : c + 1, :]
         term = innovation * innovation * jnp.concatenate([w, w], axis=1)
-        pick = jnp.where(col == 2 * p + row // obs, 1.0, 0.0).astype(BF16)
-        score[c] = score[c] + dot(side_by_side(term), jnp.concatenate([pick, pick], axis=0))
+        a, b = square_ref[c, :, 2 * p : 2 * p + 1], square_ref[c, :, 2 * p + 1 : 2 * p + 2]
+        score[c] = score[c] + term * jnp.where(first_half, a, b)
 
     for p in range(CHUNK // 2):
         both = [side_by_side(x[c]) for c in range(2)]
@@ -386,9 +385,7 @@
     for c in range(2):
         settle(c)
 
-    total = score[0] * square_ref[0] + score[1] * square_ref[1]
-    lanes = lax.broadcasted_iota(jnp.int32, (1, LANES), 1)
-    total = jnp.where(lanes < CHUNK, total, 0.0)
+    total = score[0] + score[1]
     per_batch = jnp.sum(total.reshape(blocks, per_block, LANES), axis=1)
     local = lax.dot_general(
         jnp.ones((8, 3 * LANES), BF16), jnp.concatenate(thirds(per_batch), axis=1),

time: 42.3 us -> 41.9 us (level)
  transfers between devices with their start and end apart: 4 -> 4, of which waited for: 1 -> 1; matrix products, arithmetic and copies ran while one was open for 0% -> 0% of each run, Pallas kernels for 19% -> 20%
where the time goes in v3:
time: 41.9 us; the launch traced here: 41.7 us
  starting transfers between devices  18.1 us (43%)
  Pallas kernels  17.7 us (42%)
  waiting for transfers between devices  4.65 us (11%)
  between operations  0.71 us (2%)
  other arithmetic  0.59 us (1%)
    all_to_all x1, starting transfers between devices, per_device(): lax.all_to_all(nis, 'chan', split_axis=0, concat_axis=0, tiled=True)  13.6 us
    pallas_call x1, Pallas kernels, per_device(): pl.pallas_call(before, out_shape=first, in_specs=[pl.BlockSpec(memory_spa...  5.49 us
    pallas_call x1, Pallas kernels, per_device(): pl.pallas_call(write, out_shape=jax.ShapeDtypeStruct((channels, width, fr...  4.76 us
    all_to_all x1, waiting for transfers between devices, per_device(): lax.all_to_all(nis, 'chan', split_axis=0, concat_axis=0, tiled=True)  4.64 us
    ppermute x3, starting transfers between devices, per_device(): lax.ppermute(ends, 'tm', [(i, (i + s) % sections) for i in range(sections)])  4.5 us
    pallas_call x1, Pallas kernels, per_device(): pl.pallas_call(after, out_shape=[pltpu.HBM((channels, CHUNK, chunks, widt...  4 us
    pallas_call x1, Pallas kernels, per_device(): pl.pallas_call(between, out_shape=second, in_specs=[vmem] * len(kept), ou...  3.43 us
  transfers between devices with their start and end apart: 4, of which 1 were waited for; matrix products, arithmetic and copies ran while one was open for 0% of the time, Pallas kernels for 20%

profile of v3, /device:TPU:1, one launch (start us, length us, event | category | flops | bytes accessed | tf_op | source)
XLA Modules:
  0.0 41.7 jit_solution(1659542991028430018)
XLA Ops:
  0.6 5.5 %before.1 = (f32[4,128]{1,0:T(4,128)S(1)}, f32[2,256,128]{2,1,0:T(8,128)S(1)}, f32[2,256,128]{2,1,0:T(8,128)S(1)}, bf16[2,8,256,256]{3,2,1,0:T(8,128)(2,1)S(1)},...) custom-call(f32[128,4096]{1,0:T(8,128)} %bitcast.1, ...), custom_call_target="tpu_custom_call" | custom-call | tf_op jit(solution)/shard_map/before/pallas_call | solution.py:456
  6.1 3.4 %collective-permute-start.2 = (f32[4,128]{1,0:T(4,128)S(1)}, f32[4,128]{1,0:T(4,128)S(1)}, u32[]{:S(2)}, u32[]{:S(2)}) collective-permute-start(f32[4,128]{1,0:T(4,128)S(1)} %get-tuple-element.24), channel_id=1, source_target_pairs={{0,192},{64,0},{128,64},{192,128},{1,193},{65,1},{129,65},{193,129... | collective-permute-start | bytes 6152 | tf_op jit(solution)/shard_map/ppermute | solution.py:513
  9.5 0.5 %collective-permute-start.1 = (f32[4,128]{1,0:T(4,128)S(1)}, f32[4,128]{1,0:T(4,128)S(1)}, u32[]{:S(2)}, u32[]{:S(2)}) collective-permute-start(f32[4,128]{1,0:T(4,128)S(1)} %get-tuple-element.24), channel_id=1, source_target_pairs={{0,128},{64,192},{128,0},{192,64},{1,129},{65,193},{129,1},{193,65... | collective-permute-start | bytes 6152 | tf_op jit(solution)/shard_map/ppermute | solution.py:513
  10.0 0.6 %collective-permute-start = (f32[4,128]{1,0:T(4,128)S(1)}, f32[4,128]{1,0:T(4,128)S(1)}, u32[]{:S(2)}, u32[]{:S(2)}) collective-permute-start(f32[4,128]{1,0:T(4,128)S(1)} %get-tuple-element.24), channel_id=1, source_target_pairs={{0,64},{64,128},{128,192},{192,0},{1,65},{65,129},{129,193},{193,1... | collective-permute-start | bytes 6152 | tf_op jit(solution)/shard_map/ppermute | solution.py:513
  10.6 0.0 copy-start
  10.6 3.4 %between.1 = (f32[2,256,128]{2,1,0:T(8,128)S(1)}, f32[2,256,128]{2,1,0:T(8,128)S(1)}, f32[2,256,128]{2,1,0:T(8,128)S(1)}, bf16[2,256,256]{2,1,0:T(8,128)(2,1)S(1...) custom-call(f32[2,256,128]{2,1,0:T(8,128)S(1)} %get-tuple-element.25, ...), custom_call_target="tpu_custom_call" | custom-call | flops 4000000000 | bytes 8000000 | tf_op jit(solution)/shard_map/between/pallas_call | solution.py:495
  14.1 0.0 collective-permute-done.2.three_ref
  14.1 0.0 collective-permute-done.1.two_ref
  14.1 0.0 collective-permute-done.one_ref
  14.1 0.0 copy-done
  14.1 4.0 %after.1 = (f32[2,16,256,128]{3,2,1,0:T(8,128)}, f32[64,1,32]{2,1,0:T(1,128)}) custom-call(f32[4,128]{1,0:T(4,128)S(1)} %collective-permute-done.one_ref, f32[4,128]{1,0:T(4,128)S(1)} %collective-permute-done.1.two_ref, f32[4,128]{1,0:T(4,128)S(1)} %collective-permute-done.2.three_ref, f32[2,256,128]{2,1,0:T(8,128)S(1)} %get-tuple-element.35.scan_ref, ...), custom_call_target="tpu_custom_call" | custom-call | flops 4000000000 | bytes 8000000 | tf_op jit(solution)/shard_map/after/pallas_call | solution.py:517
  18.1 13.6 %all-to-all-start = ((f32[64,1,32]{2,1,0:T(1,128)}), f32[64,1,32]{2,1,0:T(1,128)S(1)}, u32[]{:S(2)}, u32[]{:S(2)}) async-start(f32[64,1,32]{2,1,0:T(1,128)} %get-tuple-element.45), calls=%async_computation | async-start | bytes 65536 | tf_op jit(solution)/shard_map/all_to_all | solution.py:537
  31.7 4.8 %write.1 = f32[2,128,4096]{2,1,0:T(8,128)} custom-call(f32[2,16,256,128]{3,2,1,0:T(8,128)} %get-tuple-element.44.rows_ref, f32[64,128]{1,0:T(8,128)S(1)} %get-tuple-element.28.fade_ref), custom_call_target="tpu_custom_call" | custom-call | flops 4000000000 | bytes 8388608 | tf_op jit(solution)/shard_map/write/pallas_call | solution.py:538
  36.5 4.6 %all-to-all-done = f32[64,1,32]{2,1,0:T(1,128)S(1)} async-done(((f32[64,1,32]{2,1,0:T(1,128)}), f32[64,1,32]{2,1,0:T(1,128)S(1)}, u32[]{:S(2)}, u32[]{:S(2)}) %all-to-all-start) | async-done | bytes 8224 | tf_op jit(solution)/shard_map/all_to_all | solution.py:537
  41.2 0.6 %reduce_sum.9 = f32[32]{0:T(128)} reduce(f32[64,1,32]{2,1,0:T(1,128)S(1)} %all-to-all-done, f32[]{:T(128)} %constant.0.clone.1), dimensions={0,1}, to_apply=%region_0.0 | reduce | flops 2016 | bytes 8324 | tf_op jit(solution)/shard_map/reduce_sum | solution.py:555
Async XLA Ops:
  6.1 7.9 %collective-permute-start.2 = (f32[4,128]{1,0:T(4,128)S(1)}, f32[4,128]{1,0:T(4,128)S(1)}, u32[]{:S(2)}, u32[]{:S(2)}) collective-permute-start(f32[4,128]{1,0:T(4,128)S(1)} %get-tuple-element.24), channel_id=1, source_target_pairs={{0,192},{64,0},{128,64},{192,128},{1,193},{65,1},{129,65},{193,129... | collective-permute-start | bytes 6152 | tf_op jit(solution)/shard_map/ppermute | solution.py:513
  9.5 4.6 %collective-permute-start.1 = (f32[4,128]{1,0:T(4,128)S(1)}, f32[4,128]{1,0:T(4,128)S(1)}, u32[]{:S(2)}, u32[]{:S(2)}) collective-permute-start(f32[4,128]{1,0:T(4,128)S(1)} %get-tuple-element.24), channel_id=1, source_target_pairs={{0,128},{64,192},{128,0},{192,64},{1,129},{65,193},{129,1},{193,65... | collective-permute-start | bytes 6152 | tf_op jit(solution)/shard_map/ppermute | solution.py:513
  10.0 4.1 %collective-permute-start = (f32[4,128]{1,0:T(4,128)S(1)}, f32[4,128]{1,0:T(4,128)S(1)}, u32[]{:S(2)}, u32[]{:S(2)}) collective-permute-start(f32[4,128]{1,0:T(4,128)S(1)} %get-tuple-element.24), channel_id=1, source_target_pairs={{0,64},{64,128},{128,192},{192,0},{1,65},{65,129},{129,193},{193,1... | collective-permute-start | bytes 6152 | tf_op jit(solution)/shard_map/ppermute | solution.py:513
  10.6 3.5 %copy-start = (f32[2,64]{1,0:T(2,128)S(1)}, f32[2,64]{1,0:T(2,128)}, u32[]{:S(2)}) copy-start(f32[2,64]{1,0:T(2,128)} %weight_ref.1) | copy-start | bytes 1540
  18.1 23.0 %all-to-all-start = ((f32[64,1,32]{2,1,0:T(1,128)}), f32[64,1,32]{2,1,0:T(1,128)S(1)}, u32[]{:S(2)}, u32[]{:S(2)}) async-start(f32[64,1,32]{2,1,0:T(1,128)} %get-tuple-element.45), calls=%async_computation | async-start | bytes 65536 | tf_op jit(solution)/shard_map/all_to_all | solution.py:537
